TPU v7x, 32 devices: a whole 2x2x4 slice. The times are simulated.
32 devices in a mesh: hb: 4 (over y, core), row: 2 (over x), col: 4 (over z).
Axes of the slice: x: 2, y: 2, z: 4, core: 2. Of those that a mesh axis runs over, the one named last changes fastest.
Arguments:
- cell_state: float32 [256, 8, 256, 512], P('hb', None, 'row', 'col'), may hold values from -6 to 6
- normalizer: float32 [256, 8, 256], P('hb', None, 'row'), may hold values from 0.1 to 4
- stabilizer: float32 [256, 8, 16], P('hb', None, 'row'), may hold values from -5 to 120
- queries: float32 [256, 8, 256], P('hb', None, 'row'), may hold values from 0.0125 to 0.1125
- key_vectors: float32 [256, 8, 256], P('hb', None, 'row'), may hold values from -6 to 6
- token_value_vectors: float32 [256, 8, 512], P('hb', None, 'col'), may hold values from -6 to 6
- input_gate: float32 [256, 8], P('hb'), may hold values from -3 to 3
- forget_gate: float32 [256, 8], P('hb'), may hold values from -1 to 5
- output_gate_logits: float32 [256, 8, 512], P('hb', None, 'col'), may hold values from -6 to 6
- norm_gain: float32 [8, 512], P(None, 'col'), may hold values from 0.5 to 1.5
- out_weight: bfloat16 [8, 512, 4096], P('hb', 'col', 'row'), may hold values from -0.09375 to 0.09375
Outputs:
- layer_out: float32 [256, 4096], P('hb', 'row')
- readout: float32 [256, 8, 512], P('hb', None, 'col')
- refreshed_cell: float32 [256, 8, 256, 512], P('hb', None, 'row', 'col')
- new_normal: float32 [256, 8, 256], P('hb', None, 'row')
- new_stab: float32 [256, 8, 16], P('hb', None, 'row')
All inputs are finite; a program needn't handle non-finite values.
Results may differ from a plain program's by a relative error of at most 0.0029.
Values may be sent and summed in bfloat16 or wider, within the bound.
A program may use at most 128 MiB of HBM per device.

v0:
```python
import jax
import jax.numpy as jnp
from jax import lax
from jax.sharding import PartitionSpec as P

DK = 256
DV = 512
RBLK = 16


def combined_all(part, axis, combine):
    gathered = jax.tree.map(lambda a: lax.all_gather(a, axis), part)

    def take(source):
        return jax.tree.map(lambda a: lax.dynamic_index_in_dim(a, source, 0, False), gathered)

    return lax.fori_loop(
        1, lax.axis_size(axis), lambda source, state: combine(state, take(source)), take(0)
    )


def combine_pairs(left_pair, right_pair):
    joined = jnp.maximum(left_pair[0], right_pair[0])
    left_scale = jnp.exp(left_pair[0] - joined)
    right_scale = jnp.exp(right_pair[0] - joined)
    numerator = left_pair[1] * left_scale[:, :, None] + right_pair[1] * right_scale[:, :, None]
    denom = left_pair[2] * left_scale + right_pair[2] * right_scale
    return (joined, numerator, denom)


def local(
    cell_state,
    normalizer,
    stabilizer,
    queries,
    key_vectors,
    token_value_vectors,
    input_gate,
    forget_gate,
    output_gate_logits,
    norm_gain,
    out_weight,
):
    carried = jax.nn.log_sigmoid(forget_gate)[:, :, None] + stabilizer
    fresh = jnp.maximum(carried, input_gate[:, :, None])
    keep = jnp.repeat(jnp.exp(carried - fresh), RBLK, axis=2)
    admit = jnp.repeat(jnp.exp(input_gate[:, :, None] - fresh), RBLK, axis=2)
    scaled = key_vectors * DK ** (-0.5)
    refreshed_cell = (
        keep[:, :, :, None] * cell_state
        + (admit * scaled)[:, :, :, None] * token_value_vectors[:, :, None, :]
    )
    new_normal = keep * normalizer + admit * scaled
    local_top = jnp.max(fresh, axis=2)
    weight_matrix = jnp.repeat(jnp.exp(fresh - local_top[:, :, None]), RBLK, axis=2) * queries
    numerator = jnp.einsum(
        "bhkv,bhk->bhv", refreshed_cell, weight_matrix, precision=lax.Precision.HIGHEST
    )
    denom = jnp.sum(new_normal * weight_matrix, axis=2)
    top, numerator, denom = combined_all((local_top, numerator, denom), "row", combine_pairs)
    readout = numerator / jnp.maximum(jnp.abs(denom), jnp.exp(-top))[:, :, None]
    running_totals, squares = lax.psum(
        (jnp.sum(readout, axis=2), jnp.sum(readout * readout, axis=2)), "col"
    )
    mean = running_totals / DV
    var = squares / DV - mean * mean
    normed = (readout - mean[:, :, None]) * lax.rsqrt(var + 1e-06)[:, :, None]
    gated = (normed * norm_gain * jax.nn.sigmoid(output_gate_logits)).astype(jnp.bfloat16)
    seq_rows = gated.shape[0]
    out_cols = out_weight.shape[2]
    partial_value = jnp.dot(
        gated.reshape(seq_rows, -1),
        lax.all_gather(out_weight, "hb", axis=0, tiled=True).reshape(-1, out_cols),
        preferred_element_type=jnp.float32,
    )
    layer_out = lax.psum(partial_value, "col")
    return (layer_out, readout, refreshed_cell, new_normal, fresh)


def solution(mesh):
    placed = (
        P("hb", None, "row", "col"),
        P("hb", None, "row"),
        P("hb", None, "row"),
        P("hb", None, "row"),
        P("hb", None, "row"),
        P("hb", None, "col"),
        P("hb", None),
        P("hb", None),
        P("hb", None, "col"),
        P(None, "col"),
        P("hb", "col", "row"),
    )
    return jax.shard_map(
        local,
        mesh=mesh,
        in_specs=placed,
        out_specs=(
            P("hb", "row"),
            P("hb", None, "col"),
            P("hb", None, "row", "col"),
            P("hb", None, "row"),
            P("hb", None, "row"),
        ),
        check_vma=False,
    )
```

profile of v0, /device:TPU:0, one launch (start us, length us, event | category | flops | bytes accessed | tf_op | source)
XLA Modules:
  0.0 149.9 jit_solution(2049567945831490192)
XLA Ops:
  7.2 0.0 all-gather.7.cloned.1.call-start
  7.2 0.7 all-gather.7.cloned.1.call-update
  7.9 0.0 all-reduce.3.cloned.1.call-start
  7.9 0.7 fusion.3
  8.6 0.8 fusion.12
  9.5 0.0 copy-start.2
  9.5 0.8 subtract_exponential_fusion.1
  10.3 0.2 copy.55
  10.5 1.2 copy.61
  11.7 1.2 copy.58
  12.8 1.2 copy.56
  14.0 0.2 multiply_reduce_fusion
  14.2 5.3 %all-gather.3 = f32[2,64,8]{1,2,0:T(8,128)S(1)} all-gather(f32[1,64,8]{1,2,0:T(8,128)S(1)} %bitcast.66), channel_id=3, replica_groups=mesh['hb'=4,'row'=2,'col'=4] {'row'}, dimensions={0}, use_global_device_ids=true | all-gather | bytes 6144 | tf_op jit(solution)/shard_map/all_gather | solution.py:12
  19.5 4.3 %all-gather.4 = f32[2,64,8]{1,2,0:T(8,128)S(1)} all-gather(f32[1,64,8]{1,2,0:T(8,128)S(1)} %bitcast.67), channel_id=4, replica_groups=mesh['hb'=4,'row'=2,'col'=4] {'row'}, dimensions={0}, use_global_device_ids=true | all-gather | bytes 6144 | tf_op jit(solution)/shard_map/all_gather | solution.py:12
  23.9 0.1 copy.59
  24.0 0.1 copy.62
  24.1 0.1 copy.60
  24.1 0.2 copy.69
  24.4 0.2 copy.57
  24.6 23.3 %multiply_add_fusion = f32[64,8,128,128]{3,2,1,0:T(8,128)} fusion(f32[64,8,128,128]{3,2,1,0:T(8,128)} %param.11, f32[64,8,128]{2,1,0:T(8,128)} %param.16, f32[64,8,128]{2,1,0:T(8,128)S(1)} %copy.57, f32[64,8,128]{2,1,0:T(8,128)S(1)} %copy.55), kind=kLoop, calls=%fused_computation | loop fusion | flops 25165824 | bytes 67895296 | tf_op jit(solution)/shard_map/add | solution.py:50
  47.9 0.0 copy-done.2
  47.9 0.0 copy-start.1
  47.9 0.0 copy-start.3
  47.9 31.9 %fusion.13 = f32[64,8,1,128]{3,2,1,0:T(1,128)S(1)} fusion(f32[64,8,128,128]{3,2,1,0:T(8,128)} %multiply_add_fusion, f32[64,8,128,1]{2,3,1,0:T(1,128)S(1)} %copy.69), kind=kOutput, calls=%fused_computation.35 | convolution fusion | flops 100663296 | bytes 34078720 | tf_op jit(solution)/shard_map/bhkv,bhk->bhv/dot_general | solution.py:56
  79.9 7.0 %all-gather = f32[128,8,128]{2,1,0:T(8,128)S(1)} all-gather(f32[64,8,128]{2,1,0:T(8,128)S(1)} %bitcast.65), channel_id=2, replica_groups=mesh['hb'=4,'row'=2,'col'=4] {'row'}, dimensions={0}, use_global_device_ids=true | all-gather | bytes 786432 | tf_op jit(solution)/shard_map/all_gather | solution.py:12
  86.9 0.4 fusion.10
  87.3 0.0 copy-start
  87.4 0.1 copy.63
  87.4 0.1 copy.65
  87.5 12.7 %all-reduce = (f32[64,8]{0,1:T(8,128)S(1)}, f32[64,8]{0,1:T(8,128)S(1)}) all-reduce(f32[64,8]{0,1:T(8,128)S(1)} %copy.65, f32[64,8]{0,1:T(8,128)S(1)} %copy.63), channel_id=1, replica_groups=mesh['hb'=4,'row'=2,'col'=4] {'col'}, use_global_device_ids=true, to_apply=%region_5.6 | all-reduce | flops 1024 | bytes 8192 | tf_op jit(solution)/shard_map/psum | solution.py:62
  100.2 0.1 copy.64
  100.3 0.1 copy.66
  100.4 0.0 copy-done.1
  100.4 0.0 copy-done.3
  100.4 0.2 multiply_convert_fusion
  100.6 0.0 all-gather.7.cloned.1.call-done
  100.7 3.8 %convolution_bitcast_fusion = f32[64,2048]{1,0:T(8,128)} fusion(bf16[8,128,2048]{2,1,0:T(8,128)(2,1)} %all-gather.7.cloned.1.call-done, bf16[64,8,128]{2,1,0:T(8,128)(2,1)S(1)} %multiply_convert_fusion), kind=kOutput, calls=%fused_computation.1 | convolution fusion | flops 268435456 | bytes 4849664 | tf_op jit(solution)/shard_map/dot_general | solution.py:71
  104.5 0.0 all-reduce.3.cloned.1.call-update
  104.5 0.9 copy.68
  105.4 35.8 %all-reduce.3.cloned.1.call-done = f32[64,2048]{1,0:T(8,128)} async-done(((f32[64,2048]{1,0:T(8,128)}), f32[64,2048]{1,0:T(8,128)}) %all-reduce.3.cloned.1.call-update) | async-done | bytes 524304 | tf_op jit(solution)/shard_map/psum | solution.py:76
  141.2 1.9 %copy.74 = f32[64,2048]{1,0:T(8,128)} copy(f32[64,2048]{1,0:T(8,128)} %all-reduce.3.cloned.1.call-done) | data formatting | bytes 1048576
  143.1 0.0 copy-done
  (3 shorter events, 0.1 us)
Async XLA Ops:
  7.2 93.5 %all-gather.7.cloned.1.call-start = ((), (), s32[]{:S(2)}) async-start(), calls=%async_computation | async-start | bytes 5242880 | tf_op jit(solution)/shard_map/all_gather | solution.py:73
  7.9 133.3 %all-reduce.3.cloned.1.call-start = ((), (), s32[]{:S(2)}) async-start(), calls=%async_computation.1 | async-start | bytes 1048576 | tf_op jit(solution)/shard_map/psum | solution.py:76
  9.5 38.5 %copy-start.2 = (f32[64,8,8]{0,2,1:T(8,128)}, f32[64,8,8]{0,2,1:T(8,128)S(1)}, u32[]{:S(2)}) copy-start(f32[64,8,8]{0,2,1:T(8,128)S(1)} %get-tuple-element.72) | copy-start | bytes 49156
  47.9 52.5 %copy-start.1 = (f32[64,8,128]{2,1,0:T(8,128)S(1)}, f32[64,8,128]{2,1,0:T(8,128)}, u32[]{:S(2)}) copy-start(f32[64,8,128]{2,1,0:T(8,128)} %param.19) | copy-start | bytes 786436
  47.9 52.5 %copy-start.3 = (f32[8,128]{1,0:T(8,128)S(1)}, f32[8,128]{1,0:T(8,128)}, u32[]{:S(2)}) copy-start(f32[8,128]{1,0:T(8,128)} %param.20) | copy-start | bytes 12292
  87.3 55.7 %copy-start = (f32[64,8,128]{2,1,0:T(8,128)}, f32[64,8,128]{2,1,0:T(8,128)S(1)}, u32[]{:S(2)}) copy-start(f32[64,8,128]{2,1,0:T(8,128)S(1)} %get-tuple-element.69) | copy-start | bytes 786436
Sparse Core Ops, SparseCore 0:
  9.5 37.1 all-gather.6
  104.6 36.5 all-reduce.2
where the time goes:
time: 150 us
  waiting for transfers between devices  36.5 us (24%)
  matrix products  35.8 us (24%)
  blocking collectives  29.4 us (20%)
  other arithmetic  26.5 us (18%)
  between operations  14.2 us (9%)
  local copies, waits for them, and re-layouts  7.43 us (5%)
    psum x1, waiting for transfers between devices, local(): layer_out = lax.psum(partial_value, 'col')  35.8 us
    dot_general x1, matrix products, local(): jnp.einsum('bhkv,bhk->bhv', refreshed_cell, weight_matrix, precision=lax....  31.9 us
    add x1, other arithmetic, local(): keep[:, :, :, None] * cell_state  23.3 us
    all_gather x3, blocking collectives, combined_all(): gathered = jax.tree.map(lambda a: lax.all_gather(a, axis), part)  16.7 us
    psum x1, blocking collectives, local(): lax.psum((jnp.sum(readout, axis=2), jnp.sum(readout * readout, axis=2)),...  12.7 us
    unnamed x13, local copies, waits for them, and re-layouts  6.25 us
    dot_general x1, matrix products, local(): jnp.dot(gated.reshape(seq_rows, -1), lax.all_gather(out_weight, 'hb', axi...  3.83 us
  transfers between devices with their start and end apart: 2, of which 1 were waited for; matrix products, arithmetic and copies ran while one was open for 43% of the time, Pallas kernels for 0%

commit v1 on v0

--- a/solution.py
+++ b/solution.py
@@ -73,7 +73,11 @@
         lax.all_gather(out_weight, "hb", axis=0, tiled=True).reshape(-1, out_cols),
         preferred_element_type=jnp.float32,
     )
-    layer_out = lax.psum(partial_value, "col")
+    layer_out = partial_value
+    for hop in (1, 2):
+        layer_out = layer_out + lax.ppermute(
+            layer_out, "col", [(dev, dev ^ hop) for dev in range(4)]
+        )
     return (layer_out, readout, refreshed_cell, new_normal, fresh)
 
 

time: 150 us -> 140 us (0.933)
  waiting for transfers between devices: 36.5 us -> 27.8 us
  local copies, waits for them, and re-layouts: 7.43 us -> 5.55 us
    psum x1 -> x0, waiting for transfers between devices: 35.8 us -> none  [local(): layer_out = lax.psum(partial_value, 'col')]
    ppermute x0 -> x2, waiting for transfers between devices: none -> 27.1 us  [local(): lax.ppermute(layer_out, 'col', [(dev, dev ^ hop) for dev in range(4)])]
    unnamed x13 -> x12, local copies, waits for them, and re-layouts: 6.25 us -> 4.38 us
  transfers between devices with their start and end apart: 2 -> 3, of which waited for: 1 -> 2; matrix products, arithmetic and copies ran while one was open for 43% -> 46% of each run, Pallas kernels for 0% -> 0%
where the time goes in v1:
time: 140 us
  matrix products  35 us (25%)
  blocking collectives  29.5 us (21%)
  waiting for transfers between devices  27.8 us (20%)
  other arithmetic  27.5 us (20%)
  between operations  14.2 us (10%)
  local copies, waits for them, and re-layouts  5.55 us (4%)
    dot_general x1, matrix products, local(): jnp.einsum('bhkv,bhk->bhv', refreshed_cell, weight_matrix, precision=lax....  31.9 us
    ppermute x2, waiting for transfers between devices, local(): lax.ppermute(layer_out, 'col', [(dev, dev ^ hop) for dev in range(4)])  27.1 us
    add x1, other arithmetic, local(): keep[:, :, :, None] * cell_state  23.3 us
    all_gather x3, blocking collectives, combined_all(): gathered = jax.tree.map(lambda a: lax.all_gather(a, axis), part)  16.7 us
    psum x1, blocking collectives, local(): lax.psum((jnp.sum(readout, axis=2), jnp.sum(readout * readout, axis=2)),...  12.8 us
    unnamed x12, local copies, waits for them, and re-layouts  4.38 us
    dot_general x1, matrix products, local(): jnp.dot(gated.reshape(seq_rows, -1), lax.all_gather(out_weight, 'hb', axi...  3.03 us
  transfers between devices with their start and end apart: 3, of which 2 were waited for; matrix products, arithmetic and copies ran while one was open for 46% of the time, Pallas kernels for 0%

profile of v1, /device:TPU:0, one launch (start us, length us, event | category | flops | bytes accessed | tf_op | source)
XLA Modules:
  0.0 139.6 jit_solution(6251009202760472372)
XLA Ops:
  7.2 0.0 all-gather.7.cloned.1.call-start
  7.2 0.7 all-gather.7.cloned.1.call-update
  7.9 0.7 fusion.3
  8.6 0.8 fusion.12
  9.4 0.0 copy-start.2
  9.4 0.8 subtract_exponential_fusion.1
  10.3 0.2 copy.55
  10.5 1.2 copy.61
  11.6 1.2 copy.58
  12.8 1.2 copy.56
  14.0 0.2 multiply_reduce_fusion
  14.2 5.3 %all-gather.3 = f32[2,64,8]{1,2,0:T(8,128)S(1)} all-gather(f32[1,64,8]{1,2,0:T(8,128)S(1)} %bitcast.66), channel_id=3, replica_groups=mesh['hb'=4,'row'=2,'col'=4] {'row'}, dimensions={0}, use_global_device_ids=true | all-gather | bytes 6144 | tf_op jit(solution)/shard_map/all_gather | solution.py:12
  19.5 4.3 %all-gather.4 = f32[2,64,8]{1,2,0:T(8,128)S(1)} all-gather(f32[1,64,8]{1,2,0:T(8,128)S(1)} %bitcast.67), channel_id=4, replica_groups=mesh['hb'=4,'row'=2,'col'=4] {'row'}, dimensions={0}, use_global_device_ids=true | all-gather | bytes 6144 | tf_op jit(solution)/shard_map/all_gather | solution.py:12
  23.8 0.1 copy.59
  23.9 0.1 copy.62
  24.0 0.1 copy.60
  24.1 0.2 copy.69
  24.3 0.2 copy.57
  24.5 23.3 %multiply_add_fusion = f32[64,8,128,128]{3,2,1,0:T(8,128)} fusion(f32[64,8,128,128]{3,2,1,0:T(8,128)} %param.11, f32[64,8,128]{2,1,0:T(8,128)} %param.16, f32[64,8,128]{2,1,0:T(8,128)S(1)} %copy.57, f32[64,8,128]{2,1,0:T(8,128)S(1)} %copy.55), kind=kLoop, calls=%fused_computation | loop fusion | flops 25165824 | bytes 67895296 | tf_op jit(solution)/shard_map/add | solution.py:50
  47.8 0.0 copy-done.2
  47.9 0.0 copy-start.1
  47.9 0.0 copy-start.3
  47.9 31.9 %fusion.13 = f32[64,8,1,128]{3,2,1,0:T(1,128)S(1)} fusion(f32[64,8,128,128]{3,2,1,0:T(8,128)} %multiply_add_fusion, f32[64,8,128,1]{2,3,1,0:T(1,128)S(1)} %copy.69), kind=kOutput, calls=%fused_computation.35 | convolution fusion | flops 100663296 | bytes 34078720 | tf_op jit(solution)/shard_map/bhkv,bhk->bhv/dot_general | solution.py:56
  79.8 7.0 %all-gather = f32[128,8,128]{2,1,0:T(8,128)S(1)} all-gather(f32[64,8,128]{2,1,0:T(8,128)S(1)} %bitcast.65), channel_id=2, replica_groups=mesh['hb'=4,'row'=2,'col'=4] {'row'}, dimensions={0}, use_global_device_ids=true | all-gather | bytes 786432 | tf_op jit(solution)/shard_map/all_gather | solution.py:12
  86.9 0.4 fusion.10
  87.3 0.0 copy-start
  87.3 0.1 copy.63
  87.4 0.1 copy.65
  87.4 12.8 %all-reduce = (f32[64,8]{0,1:T(8,128)S(1)}, f32[64,8]{0,1:T(8,128)S(1)}) all-reduce(f32[64,8]{0,1:T(8,128)S(1)} %copy.65, f32[64,8]{0,1:T(8,128)S(1)} %copy.63), channel_id=1, replica_groups=mesh['hb'=4,'row'=2,'col'=4] {'col'}, use_global_device_ids=true, to_apply=%region_5.6 | all-reduce | flops 1024 | bytes 8192 | tf_op jit(solution)/shard_map/psum | solution.py:62
  100.3 0.1 copy.64
  100.3 0.1 copy.66
  100.4 0.0 copy-done.1
  100.4 0.0 copy-done.3
  100.4 0.2 multiply_convert_fusion
  100.6 0.0 all-gather.7.cloned.1.call-done
  100.7 3.0 %convolution_bitcast_fusion = f32[64,2048]{1,0:T(8,128)S(1)} fusion(bf16[8,128,2048]{2,1,0:T(8,128)(2,1)} %all-gather.7.cloned.1.call-done, bf16[64,8,128]{2,1,0:T(8,128)(2,1)S(1)} %multiply_convert_fusion), kind=kOutput, calls=%fused_computation.1 | convolution fusion | flops 268435456 | bytes 4849664 | tf_op jit(solution)/shard_map/dot_general | solution.py:71
  103.7 0.1 collective-permute-start
  103.8 11.7 %collective-permute-done = f32[64,2048]{1,0:T(8,128)S(1)} collective-permute-done((f32[64,2048]{1,0:T(8,128)S(1)}, f32[64,2048]{1,0:T(8,128)S(1)}, u32[]{:S(2)}, u32[]{:S(2)}) %collective-permute-start) | collective-permute-done | bytes 524320 | tf_op jit(solution)/shard_map/ppermute | solution.py:78
  115.5 0.1 add.73
  115.6 0.1 collective-permute-start.1
  115.7 0.9 copy.68
  116.5 15.4 %collective-permute-done.1 = f32[64,2048]{1,0:T(8,128)S(1)} collective-permute-done((f32[64,2048]{1,0:T(8,128)S(1)}, f32[64,2048]{1,0:T(8,128)S(1)}, u32[]{:S(2)}, u32[]{:S(2)}) %collective-permute-start.1) | collective-permute-done | bytes 524320 | tf_op jit(solution)/shard_map/ppermute | solution.py:78
  131.9 0.8 add.74
  132.8 0.0 copy-done
  (3 shorter events, 0.1 us)
Async XLA Ops:
  7.2 93.5 %all-gather.7.cloned.1.call-start = ((), (), s32[]{:S(2)}) async-start(), calls=%async_computation | async-start | bytes 5242880 | tf_op jit(solution)/shard_map/all_gather | solution.py:73
  9.4 38.4 %copy-start.2 = (f32[64,8,8]{0,2,1:T(8,128)}, f32[64,8,8]{0,2,1:T(8,128)S(1)}, u32[]{:S(2)}) copy-start(f32[64,8,8]{0,2,1:T(8,128)S(1)} %get-tuple-element.59) | copy-start | bytes 49156
  47.9 52.6 %copy-start.1 = (f32[64,8,128]{2,1,0:T(8,128)S(1)}, f32[64,8,128]{2,1,0:T(8,128)}, u32[]{:S(2)}) copy-start(f32[64,8,128]{2,1,0:T(8,128)} %param.19) | copy-start | bytes 786436
  47.9 52.6 %copy-start.3 = (f32[8,128]{1,0:T(8,128)S(1)}, f32[8,128]{1,0:T(8,128)}, u32[]{:S(2)}) copy-start(f32[8,128]{1,0:T(8,128)} %param.20) | copy-start | bytes 12292
  87.3 45.5 %copy-start = (f32[64,8,128]{2,1,0:T(8,128)}, f32[64,8,128]{2,1,0:T(8,128)S(1)}, u32[]{:S(2)}) copy-start(f32[64,8,128]{2,1,0:T(8,128)S(1)} %get-tuple-element.53) | copy-start | bytes 786436
  103.7 11.8 %collective-permute-start = (f32[64,2048]{1,0:T(8,128)S(1)}, f32[64,2048]{1,0:T(8,128)S(1)}, u32[]{:S(2)}, u32[]{:S(2)}) collective-permute-start(f32[64,2048]{1,0:T(8,128)S(1)} %convolution_bitcast_fusion), channel_id=1, source_target_pairs={{0,1},{1,0},{2,3},{3,2},{4,5},{5,4},{6,7},{7,6},{8,9},{9,8},{10,11... | collective-permute-start | bytes 1572872 | tf_op jit(solution)/shard_map/ppermute | solution.py:78
  115.6 16.4 %collective-permute-start.1 = (f32[64,2048]{1,0:T(8,128)S(1)}, f32[64,2048]{1,0:T(8,128)S(1)}, u32[]{:S(2)}, u32[]{:S(2)}) collective-permute-start(f32[64,2048]{1,0:T(8,128)S(1)} %add.73), channel_id=1, source_target_pairs={{0,2},{1,3},{2,0},{3,1},{4,6},{5,7},{6,4},{7,5},{8,10},{9,11},{10,... | collective-permute-start | bytes 1572872 | tf_op jit(solution)/shard_map/ppermute | solution.py:78
Sparse Core Ops, SparseCore 0:
  9.5 37.1 all-gather.6
